TPU v7x, 32 devices: a whole 2x2x4 slice. The times are simulated.
32 devices in a mesh: frame: 4 (over y, core), row: 8 (over z, x).
Axes of the slice: x: 2, y: 2, z: 4, core: 2. Of those that a mesh axis runs over, the one named last changes fastest.
Arguments:
- features: float32 [4, 32, 256, 256], P('frame', 'row'), may hold values from -6 to 6
- conv_weight: float32 [2, 3, 3, 256, 256], replicated, may hold values from -0.125 to 0.125
Outputs:
- activations: float32 [4, 32, 256, 256], P('frame', 'row')
All inputs are finite; a program needn't handle non-finite values.
Results may differ from a plain program's by a relative error of at most 0.0001.
Values sent between devices are 32-bit elements; how exact they have to be, the bound alone decides.
A program may use at most 64 MiB of HBM per device.

v0:
```python
import jax
import jax.numpy as jnp
from jax import lax
from jax.sharding import PartitionSpec as P

LAYERS = 2


def passed_along(block, axis, distance):
    devices = range(lax.axis_size(axis))
    route = [(i - distance, i) for i in devices if i - distance in devices]
    return lax.ppermute(block, axis, route)


def padded_2(cells, sides, width):
    for axis, dim in sides:
        count = lax.axis_size(axis)
        ends = count - 1
        head = lax.slice_in_dim(cells, 0, width, axis=dim)
        tail = lax.slice_in_dim(cells, cells.shape[dim] - width, cells.shape[dim], axis=dim)
        cells = jnp.concatenate(
            [
                lax.ppermute(tail, axis, [(i, (i + 1) % count) for i in range(ends)]),
                cells,
                lax.ppermute(head, axis, [((i + 1) % count, i) for i in range(ends)]),
            ],
            axis=dim,
        )
    return cells


def convolve_block(padded, kernel):
    frames, rows_pad, cols, chans = padded.shape
    rows = rows_pad - 2
    widened = jnp.pad(padded, ((0, 0), (0, 0), (1, 1), (0, 0)))
    total = jnp.zeros((frames * rows * cols, kernel.shape[3]), jnp.float32)
    for tap_row in range(3):
        for tap_col in range(3):
            window = widened[:, tap_row : tap_row + rows, tap_col : tap_col + cols, :].reshape(
                frames * rows * cols, chans
            )
            total = total + jnp.dot(
                window,
                kernel[tap_row, tap_col],
                preferred_element_type=jnp.float32,
                precision=lax.Precision.HIGHEST,
            )
    return jnp.maximum(total, 0.0).reshape(frames, rows, cols, kernel.shape[3])


def shift_layer(field, kernel):
    fold = field.shape[3] // 8
    incoming_next = passed_along(field[:1, :, :, :fold], "frame", -1)
    incoming_prev = passed_along(field[-1:, :, :, fold : 2 * fold], "frame", 1)
    from_next = jnp.concatenate([field[1:, :, :, :fold], incoming_next], axis=0)
    from_prev = jnp.concatenate([incoming_prev, field[:-1, :, :, fold : 2 * fold]], axis=0)
    shifted = jnp.concatenate([from_next, from_prev, field[:, :, :, 2 * fold :]], axis=3)
    padded = padded_2(shifted, (("row", 1),), 1)
    return convolve_block(padded, kernel)


def local(features, conv_weight):
    field = features
    for layer in range(LAYERS):
        field = shift_layer(field, conv_weight[layer])
    return field


def solution(mesh):
    placed = (P("frame", "row", None, None), P())
    return jax.shard_map(
        local, mesh=mesh, in_specs=placed, out_specs=P("frame", "row", None, None), check_vma=False
    )
```

profile of v0, /device:TPU:14, one launch (start us, length us, event | category | flops | bytes accessed | tf_op | source)
XLA Modules:
  0.0 75.5 jit_solution(16911610871237954720)
XLA Ops:
  0.0 1.5 %fusion.30 = (f32[1,4,256,32]{3,2,1,0:T(8,128)S(1)}, f32[1,4,256,32]{3,2,1,0:T(8,128)S(1)}) fusion(f32[1,4,256,256]{3,2,1,0:T(8,128)} %param.2), kind=kLoop, calls=%fused_computation.76 | loop fusion | bytes 524288 | tf_op jit(solution)/shard_map/slice | solution.py:53
  1.5 1.9 %collective-permute-start = (f32[1,4,256,32]{3,2,1,0:T(8,128)S(1)}, f32[1,4,256,32]{3,2,1,0:T(8,128)S(1)}, u32[]{:S(2)}, u32[]{:S(2)}) collective-permute-start(f32[1,4,256,32]{3,2,1,0:T(8,128)S(1)} %get-tuple-element.29), channel_id=1, source_target_pairs={{8,0},{16,8},{24,16},{9,1},{17,9},{25,17},{10,2},{18,10},{26,18},{... | collective-permute-start | bytes 393224 | tf_op jit(solution)/shard_map/ppermute | solution.py:12
  3.4 2.6 %collective-permute-start.1 = (f32[1,4,256,32]{3,2,1,0:T(8,128)S(1)}, f32[1,4,256,32]{3,2,1,0:T(8,128)S(1)}, u32[]{:S(2)}, u32[]{:S(2)}) collective-permute-start(f32[1,4,256,32]{3,2,1,0:T(8,128)S(1)} %get-tuple-element.30), channel_id=1, source_target_pairs={{0,8},{8,16},{16,24},{1,9},{9,17},{17,25},{2,10},{10,18},{18,26},{... | collective-permute-start | bytes 393224 | tf_op jit(solution)/shard_map/ppermute | solution.py:12
  6.0 2.8 %slice_bitcast_fusion = (f32[3,3,256,256]{3,2,1,0:T(8,128)S(1)}, f32[3,3,256,256]{3,2,1,0:T(8,128)S(1)}) fusion(f32[2,3,3,256,256]{4,3,2,1,0:T(8,128)} %param.3), kind=kLoop, calls=%fused_computation.2 | loop fusion | bytes 9437184 | tf_op jit(solution)/shard_map/squeeze | solution.py:65
  10.1 4.0 %collective-permute-done.1 = f32[1,4,256,32]{3,2,1,0:T(8,128)S(1)} collective-permute-done((f32[1,4,256,32]{3,2,1,0:T(8,128)S(1)}, f32[1,4,256,32]{3,2,1,0:T(8,128)S(1)}, u32[]{:S(2)}, u32[]{:S(2)}) %collective-permute-start.1) | collective-permute-done | bytes 131104 | tf_op jit(solution)/shard_map/ppermute | solution.py:12
  14.7 3.5 %collective-permute-start.2 = (f32[1,1,256,256]{3,2,1,0:T(8,128)S(1)}, f32[1,1,256,256]{3,2,1,0:T(8,128)S(1)}, u32[]{:S(2)}, u32[]{:S(2)}) collective-permute-start(f32[1,1,256,256]{3,2,1,0:T(8,128)S(1)} %get-tuple-element.27), channel_id=1, source_target_pairs={{0,1},{1,2},{2,3},{3,4},{4,5},{5,6},{6,7},{8,9},{9,10},{10,11},{11... | collective-permute-start | bytes 786440 | tf_op jit(solution)/shard_map/ppermute | solution.py:23
  18.2 2.4 %collective-permute-start.3 = (f32[1,1,256,256]{3,2,1,0:T(8,128)S(1)}, f32[1,1,256,256]{3,2,1,0:T(8,128)S(1)}, u32[]{:S(2)}, u32[]{:S(2)}) collective-permute-start(f32[1,1,256,256]{3,2,1,0:T(8,128)S(1)} %get-tuple-element.28), channel_id=1, source_target_pairs={{1,0},{2,1},{3,2},{4,3},{5,4},{6,5},{7,6},{9,8},{10,9},{11,10},{12... | collective-permute-start | bytes 786440 | tf_op jit(solution)/shard_map/ppermute | solution.py:25
  21.6 1.9 %collective-permute-done.2 = f32[1,1,256,256]{3,2,1,0:T(8,128)S(1)} collective-permute-done((f32[1,1,256,256]{3,2,1,0:T(8,128)S(1)}, f32[1,1,256,256]{3,2,1,0:T(8,128)S(1)}, u32[]{:S(2)}, u32[]{:S(2)}) %collective-permute-start.2) | collective-permute-done | bytes 262176 | tf_op jit(solution)/shard_map/ppermute | solution.py:23
  23.4 3.9 %collective-permute-done.3 = f32[1,1,256,256]{3,2,1,0:T(8,128)S(1)} collective-permute-done((f32[1,1,256,256]{3,2,1,0:T(8,128)S(1)}, f32[1,1,256,256]{3,2,1,0:T(8,128)S(1)}, u32[]{:S(2)}, u32[]{:S(2)}) %collective-permute-start.3) | collective-permute-done | bytes 262176 | tf_op jit(solution)/shard_map/ppermute | solution.py:25
  28.6 1.0 %fusion.17 = f32[1024,256]{1,0:T(8,128)S(1)} fusion(f32[1024,256]{1,0:T(8,128)S(1)} %bitcast.108, f32[3,3,256,256]{3,2,1,0:T(8,128)S(1)} %get-tuple-element.6), kind=kOutput, calls=%fused_computation.55 | convolution fusion | flops 805306368 | bytes 2359296 | tf_op jit(solution)/shard_map/dot_general | solution.py:42
  32.5 1.0 %fusion.21 = f32[1024,256]{1,0:T(8,128)S(1)} fusion(f32[1024,256]{1,0:T(8,128)S(1)} %bitcast.102, f32[3,3,256,256]{3,2,1,0:T(8,128)S(1)} %get-tuple-element.6), kind=kOutput, calls=%fused_computation.64 | convolution fusion | flops 805306368 | bytes 2359296 | tf_op jit(solution)/shard_map/dot_general | solution.py:42
  35.5 1.0 %fusion.24 = f32[1024,256]{1,0:T(8,128)S(1)} fusion(f32[1024,256]{1,0:T(8,128)S(1)} %bitcast.100, f32[3,3,256,256]{3,2,1,0:T(8,128)S(1)} %get-tuple-element.6), kind=kOutput, calls=%fused_computation.70 | convolution fusion | flops 805306368 | bytes 2359296 | tf_op jit(solution)/shard_map/dot_general | solution.py:42
  36.5 1.4 %fusion.8 = f32[1024,256]{1,0:T(8,128)S(1)} fusion(f32[1024,256]{1,0:T(8,128)S(1)} %fusion.17, f32[1024,256]{1,0:T(8,128)S(1)} %fusion.18, f32[1024,256]{1,0:T(8,128)S(1)} %fusion.19, f32[1024,256]{1,0:T(8,128)S(1)} %bitcast.114, f32[1024,256]{1,0:T(8,128)S(1)} %fusion.20, f32[1024,256]{1,0:T(8,128)S(1)} %fusion.21, f32[1024,256]{1,0:T(8,128)S(1)} %fusion.22, ...), kind=kOutput, calls=%fused_computation.22 | convolution fusion | flops 807665664 | bytes 10747904 | tf_op jit(solution)/shard_map/dot_general | solution.py:42
  38.1 1.9 %collective-permute-start.4 = (f32[1,4,256,32]{3,2,1,0:T(8,128)S(1)}, f32[1,4,256,32]{3,2,1,0:T(8,128)S(1)}, u32[]{:S(2)}, u32[]{:S(2)}) collective-permute-start(f32[1,4,256,32]{3,2,1,0:T(8,128)S(1)} %get-tuple-element.25), channel_id=1, source_target_pairs={{8,0},{16,8},{24,16},{9,1},{17,9},{25,17},{10,2},{18,10},{26,18},{... | collective-permute-start | bytes 393224 | tf_op jit(solution)/shard_map/ppermute | solution.py:12
  40.1 2.6 %collective-permute-start.5 = (f32[1,4,256,32]{3,2,1,0:T(8,128)S(1)}, f32[1,4,256,32]{3,2,1,0:T(8,128)S(1)}, u32[]{:S(2)}, u32[]{:S(2)}) collective-permute-start(f32[1,4,256,32]{3,2,1,0:T(8,128)S(1)} %get-tuple-element.26), channel_id=1, source_target_pairs={{0,8},{8,16},{16,24},{1,9},{9,17},{17,25},{2,10},{10,18},{18,26},{... | collective-permute-start | bytes 393224 | tf_op jit(solution)/shard_map/ppermute | solution.py:12
  43.0 3.7 %collective-permute-done.4 = f32[1,4,256,32]{3,2,1,0:T(8,128)S(1)} collective-permute-done((f32[1,4,256,32]{3,2,1,0:T(8,128)S(1)}, f32[1,4,256,32]{3,2,1,0:T(8,128)S(1)}, u32[]{:S(2)}, u32[]{:S(2)}) %collective-permute-start.4) | collective-permute-done | bytes 131104 | tf_op jit(solution)/shard_map/ppermute | solution.py:12
  46.7 3.8 %collective-permute-done.5 = f32[1,4,256,32]{3,2,1,0:T(8,128)S(1)} collective-permute-done((f32[1,4,256,32]{3,2,1,0:T(8,128)S(1)}, f32[1,4,256,32]{3,2,1,0:T(8,128)S(1)}, u32[]{:S(2)}, u32[]{:S(2)}) %collective-permute-start.5) | collective-permute-done | bytes 131104 | tf_op jit(solution)/shard_map/ppermute | solution.py:12
  51.2 3.6 %collective-permute-start.6 = (f32[1,1,256,256]{3,2,1,0:T(8,128)S(1)}, f32[1,1,256,256]{3,2,1,0:T(8,128)S(1)}, u32[]{:S(2)}, u32[]{:S(2)}) collective-permute-start(f32[1,1,256,256]{3,2,1,0:T(8,128)S(1)} %get-tuple-element.23), channel_id=1, source_target_pairs={{0,1},{1,2},{2,3},{3,4},{4,5},{5,6},{6,7},{8,9},{9,10},{10,11},{11... | collective-permute-start | bytes 786440 | tf_op jit(solution)/shard_map/ppermute | solution.py:23
  54.8 2.3 %collective-permute-start.7 = (f32[1,1,256,256]{3,2,1,0:T(8,128)S(1)}, f32[1,1,256,256]{3,2,1,0:T(8,128)S(1)}, u32[]{:S(2)}, u32[]{:S(2)}) collective-permute-start(f32[1,1,256,256]{3,2,1,0:T(8,128)S(1)} %get-tuple-element.24), channel_id=1, source_target_pairs={{1,0},{2,1},{3,2},{4,3},{5,4},{6,5},{7,6},{9,8},{10,9},{11,10},{12... | collective-permute-start | bytes 786440 | tf_op jit(solution)/shard_map/ppermute | solution.py:25
  58.1 1.4 %collective-permute-done.6 = f32[1,1,256,256]{3,2,1,0:T(8,128)S(1)} collective-permute-done((f32[1,1,256,256]{3,2,1,0:T(8,128)S(1)}, f32[1,1,256,256]{3,2,1,0:T(8,128)S(1)}, u32[]{:S(2)}, u32[]{:S(2)}) %collective-permute-start.6) | collective-permute-done | bytes 262176 | tf_op jit(solution)/shard_map/ppermute | solution.py:23
  59.5 4.5 %collective-permute-done.7 = f32[1,1,256,256]{3,2,1,0:T(8,128)S(1)} collective-permute-done((f32[1,1,256,256]{3,2,1,0:T(8,128)S(1)}, f32[1,1,256,256]{3,2,1,0:T(8,128)S(1)}, u32[]{:S(2)}, u32[]{:S(2)}) %collective-permute-start.7) | collective-permute-done | bytes 262176 | tf_op jit(solution)/shard_map/ppermute | solution.py:25
  69.2 1.0 %fusion.11 = f32[1024,256]{1,0:T(8,128)S(1)} fusion(f32[1024,256]{1,0:T(8,128)S(1)} %bitcast.107, f32[3,3,256,256]{3,2,1,0:T(8,128)S(1)} %get-tuple-element.5), kind=kOutput, calls=%fused_computation.42 | convolution fusion | flops 805306368 | bytes 2359296 | tf_op jit(solution)/shard_map/dot_general | solution.py:42
  70.2 1.0 %fusion.13 = f32[1024,256]{1,0:T(8,128)S(1)} fusion(f32[1024,256]{1,0:T(8,128)S(1)} %bitcast.106, f32[3,3,256,256]{3,2,1,0:T(8,128)S(1)} %get-tuple-element.5), kind=kOutput, calls=%fused_computation.47 | convolution fusion | flops 805306368 | bytes 2359296 | tf_op jit(solution)/shard_map/dot_general | solution.py:42
  73.2 2.3 %fusion.4 = f32[1024,256]{1,0:T(8,128)} fusion(f32[1024,256]{1,0:T(8,128)S(1)} %fusion.9, f32[1024,256]{1,0:T(8,128)S(1)} %fusion.10, f32[1024,256]{1,0:T(8,128)S(1)} %fusion.11, f32[1024,256]{1,0:T(8,128)S(1)} %bitcast.115, f32[1024,256]{1,0:T(8,128)S(1)} %fusion.12, f32[1024,256]{1,0:T(8,128)S(1)} %fusion.13, f32[1024,256]{1,0:T(8,128)S(1)} %fusion.14, ...), kind=kOutput, calls=%fused_computation.17 | convolution fusion | flops 807665664 | bytes 10747904 | tf_op jit(solution)/shard_map/dot_general | solution.py:42
  (27 shorter events, 18.3 us)
Async XLA Ops:
  1.5 8.6 %collective-permute-start = (f32[1,4,256,32]{3,2,1,0:T(8,128)S(1)}, f32[1,4,256,32]{3,2,1,0:T(8,128)S(1)}, u32[]{:S(2)}, u32[]{:S(2)}) collective-permute-start(f32[1,4,256,32]{3,2,1,0:T(8,128)S(1)} %get-tuple-element.29), channel_id=1, source_target_pairs={{8,0},{16,8},{24,16},{9,1},{17,9},{25,17},{10,2},{18,10},{26,18},{... | collective-permute-start | bytes 393224 | tf_op jit(solution)/shard_map/ppermute | solution.py:12
  3.4 5.4 %copy-start = (f32[1,4,256,256]{3,2,1,0:T(8,128)S(1)}, f32[1,4,256,256]{3,2,1,0:T(8,128)}, u32[]{:S(2)}) copy-start(f32[1,4,256,256]{3,2,1,0:T(8,128)} %param.2) | copy-start | bytes 3145732
  3.4 10.6 %collective-permute-start.1 = (f32[1,4,256,32]{3,2,1,0:T(8,128)S(1)}, f32[1,4,256,32]{3,2,1,0:T(8,128)S(1)}, u32[]{:S(2)}, u32[]{:S(2)}) collective-permute-start(f32[1,4,256,32]{3,2,1,0:T(8,128)S(1)} %get-tuple-element.30), channel_id=1, source_target_pairs={{0,8},{8,16},{16,24},{1,9},{9,17},{17,25},{2,10},{10,18},{18,26},{... | collective-permute-start | bytes 393224 | tf_op jit(solution)/shard_map/ppermute | solution.py:12
  14.7 8.7 %collective-permute-start.2 = (f32[1,1,256,256]{3,2,1,0:T(8,128)S(1)}, f32[1,1,256,256]{3,2,1,0:T(8,128)S(1)}, u32[]{:S(2)}, u32[]{:S(2)}) collective-permute-start(f32[1,1,256,256]{3,2,1,0:T(8,128)S(1)} %get-tuple-element.27), channel_id=1, source_target_pairs={{0,1},{1,2},{2,3},{3,4},{4,5},{5,6},{6,7},{8,9},{9,10},{10,11},{11... | collective-permute-start | bytes 786440 | tf_op jit(solution)/shard_map/ppermute | solution.py:23
  18.2 9.2 %collective-permute-start.3 = (f32[1,1,256,256]{3,2,1,0:T(8,128)S(1)}, f32[1,1,256,256]{3,2,1,0:T(8,128)S(1)}, u32[]{:S(2)}, u32[]{:S(2)}) collective-permute-start(f32[1,1,256,256]{3,2,1,0:T(8,128)S(1)} %get-tuple-element.28), channel_id=1, source_target_pairs={{1,0},{2,1},{3,2},{4,3},{5,4},{6,5},{7,6},{9,8},{10,9},{11,10},{12... | collective-permute-start | bytes 786440 | tf_op jit(solution)/shard_map/ppermute | solution.py:25
  38.1 8.6 %collective-permute-start.4 = (f32[1,4,256,32]{3,2,1,0:T(8,128)S(1)}, f32[1,4,256,32]{3,2,1,0:T(8,128)S(1)}, u32[]{:S(2)}, u32[]{:S(2)}) collective-permute-start(f32[1,4,256,32]{3,2,1,0:T(8,128)S(1)} %get-tuple-element.25), channel_id=1, source_target_pairs={{8,0},{16,8},{24,16},{9,1},{17,9},{25,17},{10,2},{18,10},{26,18},{... | collective-permute-start | bytes 393224 | tf_op jit(solution)/shard_map/ppermute | solution.py:12
  40.1 10.5 %collective-permute-start.5 = (f32[1,4,256,32]{3,2,1,0:T(8,128)S(1)}, f32[1,4,256,32]{3,2,1,0:T(8,128)S(1)}, u32[]{:S(2)}, u32[]{:S(2)}) collective-permute-start(f32[1,4,256,32]{3,2,1,0:T(8,128)S(1)} %get-tuple-element.26), channel_id=1, source_target_pairs={{0,8},{8,16},{16,24},{1,9},{9,17},{17,25},{2,10},{10,18},{18,26},{... | collective-permute-start | bytes 393224 | tf_op jit(solution)/shard_map/ppermute | solution.py:12
  51.2 8.3 %collective-permute-start.6 = (f32[1,1,256,256]{3,2,1,0:T(8,128)S(1)}, f32[1,1,256,256]{3,2,1,0:T(8,128)S(1)}, u32[]{:S(2)}, u32[]{:S(2)}) collective-permute-start(f32[1,1,256,256]{3,2,1,0:T(8,128)S(1)} %get-tuple-element.23), channel_id=1, source_target_pairs={{0,1},{1,2},{2,3},{3,4},{4,5},{5,6},{6,7},{8,9},{9,10},{10,11},{11... | collective-permute-start | bytes 786440 | tf_op jit(solution)/shard_map/ppermute | solution.py:23
  54.8 9.2 %collective-permute-start.7 = (f32[1,1,256,256]{3,2,1,0:T(8,128)S(1)}, f32[1,1,256,256]{3,2,1,0:T(8,128)S(1)}, u32[]{:S(2)}, u32[]{:S(2)}) collective-permute-start(f32[1,1,256,256]{3,2,1,0:T(8,128)S(1)} %get-tuple-element.24), channel_id=1, source_target_pairs={{1,0},{2,1},{3,2},{4,3},{5,4},{6,5},{7,6},{9,8},{10,9},{11,10},{12... | collective-permute-start | bytes 786440 | tf_op jit(solution)/shard_map/ppermute | solution.py:25
where the time goes:
time: 75.9 us; the launch traced here: 75.5 us
  waiting for transfers between devices  24 us (32%)
  starting transfers between devices  20.7 us (27%)
  matrix products  19.7 us (26%)
  local copies, waits for them, and re-layouts  6.46 us (9%)
  other arithmetic  4.32 us (6%)
    dot_general x18, matrix products, convolve_block(): jnp.dot(window, kernel[tap_row, tap_col], preferred_element_type=jnp.floa...  19.7 us
    ppermute x4, waiting for transfers between devices, passed_along(): return lax.ppermute(block, axis, route)  12.4 us
    ppermute x4, starting transfers between devices, passed_along(): return lax.ppermute(block, axis, route)  9.02 us
    ppermute x2, waiting for transfers between devices, padded_2(): lax.ppermute(head, axis, [((i + 1) % count, i) for i in range(ends)])  8.38 us
    ppermute x2, starting transfers between devices, padded_2(): lax.ppermute(tail, axis, [(i, (i + 1) % count) for i in range(ends)])  7.03 us
    ppermute x2, starting transfers between devices, padded_2(): lax.ppermute(head, axis, [((i + 1) % count, i) for i in range(ends)])  4.66 us
    ppermute x2, waiting for transfers between devices, padded_2(): lax.ppermute(tail, axis, [(i, (i + 1) % count) for i in range(ends)])  3.27 us
    concatenate x4, other arithmetic, padded_2(): jnp.concatenate([lax.ppermute(tail, axis, [(i, (i + 1) % count) for i in...  3.08 us
  transfers between devices with their start and end apart: 8, of which 8 were waited for; matrix products, arithmetic and copies ran while one was open for 7% of the time, Pallas kernels for 0%

commit v1 on v0

v1 whole, which is shorter than its diff:
```python
import functools

import jax
import jax.numpy as jnp
from jax import lax
from jax.experimental import pallas as pl
from jax.experimental.pallas import tpu as pltpu
from jax.sharding import PartitionSpec as P

MESH = pl.DeviceIdType.MESH
LANES = 128
PAD = 8


def split(value):
    high = value.astype(jnp.bfloat16)
    low = (value - high.astype(jnp.float32)).astype(jnp.bfloat16)
    return high, low


def kernel(
    cuts, x_hbm, w_hbm, o_hbm, xin, wbuf, w3, sx, acc, mid, halo, edge, pack, got, out,
    load_sem, store_sem, row_send, row_recv, frame_send, frame_recv,
):
    rows, cols, chans = xin.shape
    layers = wbuf.shape[0]
    fold = chans // 8
    last = rows - 1
    frames, bands = lax.axis_size("frame"), lax.axis_size("row")
    t, r = lax.axis_index("frame"), lax.axis_index("row")
    has_row = (r > 0, r < bands - 1)
    has_frame = (t > 0, t < frames - 1)
    row_to = (r - 1, r + 1)
    frame_to = (t - 1, t + 1)

    load_x = pltpu.make_async_copy(x_hbm.at[0], xin, load_sem.at[layers])
    load_x.start()
    load_w = [pltpu.make_async_copy(w_hbm.at[n], wbuf.at[n], load_sem.at[n]) for n in range(layers)]
    for load in load_w:
        load.start()

    barrier = pltpu.get_barrier_semaphore()
    count = 0
    for have, axis, peers in ((has_row, "row", row_to), (has_frame, "frame", frame_to)):
        for side in range(2):
            count = count + have[side].astype(jnp.int32)

            @pl.when(have[side])
            def _():
                pl.semaphore_signal(barrier, inc=1, device_id={axis: peers[side]}, device_id_type=MESH)

    pl.semaphore_wait(barrier, count)

    def maps(layer):
        return xin if layer == 0 else mid.at[layer - 1]

    def span(layer, chunk):
        return cuts[layer][chunk], cuts[layer][chunk + 1] - cuts[layer][chunk]

    def row_copy(layer, side, tile, chunk):
        start, size = span(layer, chunk)
        row = 0 if side == 0 else last
        if tile == 1:
            source = maps(layer).at[row, pl.ds(start, size), pl.ds(LANES, LANES)]
        else:
            source = edge.at[layer, side, pl.ds(start, size)]
        return pltpu.make_async_remote_copy(
            src_ref=source,
            dst_ref=halo.at[layer, 1 - side, tile, pl.ds(start, size)],
            send_sem=row_send.at[layer, side, tile, chunk],
            recv_sem=row_recv.at[layer, side, tile, chunk],
            device_id={"row": row_to[side]},
            device_id_type=MESH,
        )

    def frame_copy(layer, side, chunk):
        start, size = span(layer, chunk)
        return pltpu.make_async_remote_copy(
            src_ref=pack.at[layer, side, pl.ds(start, size)],
            dst_ref=got.at[layer, side, pl.ds(start, size)],
            send_sem=frame_send.at[layer, side, chunk],
            recv_sem=frame_recv.at[layer, side, chunk],
            device_id={"frame": frame_to[side]},
            device_id_type=MESH,
        )

    def send_rows(layer, tile, chunk):
        for side in range(2):

            @pl.when(has_row[side])
            def _():
                row_copy(layer, side, tile, chunk).start()

    def send_frames(layer, chunk):
        start, size = span(layer, chunk)
        lane = lax.broadcasted_iota(jnp.int32, (size, LANES), 1)
        for side in range(2):
            full = jnp.zeros((size, LANES), jnp.float32)
            for row in range(rows):
                value = maps(layer)[row, pl.ds(start, size), pl.ds(0, LANES)]
                shift = ((row - side) * fold) % LANES
                value = pltpu.roll(value, shift, 1) if shift else value
                full = jnp.where(lane // fold == row, value, full)
            pack[layer, side, pl.ds(start, size)] = full

            @pl.when(has_frame[side])
            def _():
                frame_copy(layer, side, chunk).start()

    def take_frames(layer, chunk):
        start, size = span(layer, chunk)
        for side in range(2):

            @pl.when(has_frame[1 - side])
            def _():
                frame_copy(layer, side, chunk).wait_recv()

            @pl.when(jnp.logical_not(has_frame[1 - side]))
            def _():
                got[layer, side, pl.ds(start, size)] = jnp.zeros((size, LANES), jnp.float32)

    def shifted_tile(layer, chunk, row):
        start, size = span(layer, chunk)
        lane = lax.broadcasted_iota(jnp.int32, (size, LANES), 1)
        value = maps(layer)[row, pl.ds(start, size), pl.ds(0, LANES)]
        for side in range(2):
            part = got[layer, side, pl.ds(start, size)]
            shift = ((side - row) * fold) % LANES
            part = pltpu.roll(part, shift, 1) if shift else part
            value = jnp.where(lane // fold == side, part, value)
        return value

    def put(row, start, size, tile, value):
        high, low = split(value)
        sx[row, pl.ds(start, size), pl.ds(tile * LANES, LANES)] = high
        sx[row, pl.ds(start, size), pl.ds(chans + tile * LANES, LANES)] = low
        sx[row, pl.ds(start, size), pl.ds(2 * chans + tile * LANES, LANES)] = high

    def lower_edges(layer, chunk):
        start, size = span(layer, chunk)
        for row in range(rows):
            value = shifted_tile(layer, chunk, row)
            if row == 0:
                edge[layer, 0, pl.ds(start, size)] = value
            if row == last:
                edge[layer, 1, pl.ds(start, size)] = value
        send_rows(layer, 0, chunk)

    def fill(layer):
        for chunk in range(len(cuts[layer]) - 1):
            start, size = span(layer, chunk)
            for row in range(rows):
                put(row + 1, start, size, 0, shifted_tile(layer, chunk, row))
                put(row + 1, start, size, 1, maps(layer)[row, pl.ds(start, size), pl.ds(LANES, LANES)])
        blank = jnp.zeros((cols, 3 * chans), jnp.bfloat16)
        sx[0] = blank
        sx[rows + 1] = blank

    def split_weights(layer):
        load_w[layer].wait()

        def tap(index, carry):
            down, across = index // 3, index % 3
            high, low = split(wbuf[layer, down, across])
            base = pl.multiple_of(down * 3 * chans, 3 * chans)
            w3[layer, across, pl.ds(base, chans)] = high
            w3[layer, across, pl.ds(base + chans, chans)] = high
            w3[layer, across, pl.ds(base + 2 * chans, chans)] = low
            return carry

        lax.fori_loop(0, 9, tap, 0)

    def inner(layer):
        def across(tap, carry):
            left = jnp.concatenate(
                [sx[pl.ds(down, rows)].reshape(rows * cols, 3 * chans) for down in range(3)], axis=1
            )
            total = jnp.dot(left, w3[layer, tap], preferred_element_type=jnp.float32)
            acc[tap, :, pl.ds(PAD, cols)] = total.reshape(rows, cols, chans)
            return carry

        lax.fori_loop(0, 3, across, 0)

    def finish(row, start, size):
        total = acc[0, row, pl.ds(PAD + start - 1, size)] + acc[1, row, pl.ds(PAD + start, size)]
        total = total + acc[2, row, pl.ds(PAD + start + 1, size)]
        return jnp.maximum(total, 0.0)

    def outer(layer, chunk):
        start, size = span(layer, chunk)
        for side in range(2):
            place = 0 if side == 0 else rows + 1

            @pl.when(has_row[side])
            def _():
                for tile in range(2):
                    row_copy(layer, 1 - side, tile, chunk).wait_recv()
                for tile in range(2):
                    put(place, start, size, tile, halo[layer, side, tile, pl.ds(start, size)])

        def across(tap, carry):
            for place, row, down in ((0, 0, 0), (rows + 1, last, 2)):
                extra = jnp.dot(
                    sx[place, pl.ds(start, size)],
                    w3[layer, tap, pl.ds(down * 3 * chans, 3 * chans)],
                    preferred_element_type=jnp.float32,
                )
                acc[tap, row, pl.ds(PAD + start, size)] += extra
            return carry

        lax.fori_loop(0, 3, across, 0)

    chunks = len(cuts[0]) - 1
    load_x.wait()
    for chunk in range(chunks):
        send_rows(0, 1, chunk)
    for chunk in range(chunks):
        send_frames(0, chunk)
    acc[:, :, pl.ds(0, PAD)] = jnp.zeros((3, rows, PAD, chans), jnp.float32)
    acc[:, :, pl.ds(PAD + cols, PAD)] = jnp.zeros((3, rows, PAD, chans), jnp.float32)
    for chunk in range(chunks):
        take_frames(0, chunk)
        lower_edges(0, chunk)
    split_weights(0)
    for layer in range(layers):
        final = layer == layers - 1
        fill(layer)
        inner(layer)
        if not final:
            split_weights(layer + 1)
        target = out if final else mid.at[layer]
        for row in range(1, last):
            target[row] = finish(row, 0, cols)
            if final:
                pltpu.make_async_copy(out.at[row], o_hbm.at[0, row], store_sem.at[row]).start()
        for chunk in range(chunks):
            outer(layer, chunk)
            start = cuts[layer + 1][chunk]
            size = cuts[layer + 1][chunk + 1] - start
            for row in (0, last):
                target[row, pl.ds(start, size)] = finish(row, start, size)
            if not final:
                send_rows(layer + 1, 1, chunk)
                send_frames(layer + 1, chunk)
                take_frames(layer + 1, chunk)
                lower_edges(layer + 1, chunk)
        if final:
            for row in (0, last):
                pltpu.make_async_copy(out.at[row], o_hbm.at[0, row], store_sem.at[row]).start()

    for layer in range(layers):
        for chunk in range(chunks):
            for side in range(2):

                @pl.when(has_row[side])
                def _():
                    for tile in range(2):
                        row_copy(layer, side, tile, chunk).wait_send()

                @pl.when(has_frame[side])
                def _():
                    frame_copy(layer, side, chunk).wait_send()

    for row in range(rows):
        pltpu.make_async_copy(out.at[row], o_hbm.at[0, row], store_sem.at[row]).wait()


def local(features, conv_weight):
    _, rows, cols, chans = features.shape
    layers = conv_weight.shape[0]
    half, step = cols // 2, 2 * PAD
    cuts = [[0, half + step * (layers - 1 - n), cols] for n in range(layers)] + [[0, half - step, cols]]
    chunks = len(cuts[0]) - 1
    f32, bf16 = jnp.float32, jnp.bfloat16
    dma = pltpu.SemaphoreType.DMA
    return pl.pallas_call(
        functools.partial(kernel, cuts),
        out_shape=jax.ShapeDtypeStruct(features.shape, f32),
        in_specs=[pl.BlockSpec(memory_space=pl.ANY)] * 2,
        out_specs=pl.BlockSpec(memory_space=pl.ANY),
        scratch_shapes=[
            pltpu.VMEM((rows, cols, chans), f32),
            pltpu.VMEM(conv_weight.shape, f32),
            pltpu.VMEM((layers, 3, 9 * chans, chans), bf16),
            pltpu.VMEM((rows + 2, cols, 3 * chans), bf16),
            pltpu.VMEM((3, rows, cols + 2 * PAD, chans), f32),
            pltpu.VMEM((layers - 1, rows, cols, chans), f32),
            pltpu.VMEM((layers, 2, 2, cols, LANES), f32),
            pltpu.VMEM((layers, 2, cols, LANES), f32),
            pltpu.VMEM((layers, 2, cols, LANES), f32),
            pltpu.VMEM((layers, 2, cols, LANES), f32),
            pltpu.VMEM((rows, cols, chans), f32),
            dma((layers + 1,)),
            dma((rows,)),
            dma((layers, 2, 2, chunks)),
            dma((layers, 2, 2, chunks)),
            dma((layers, 2, chunks)),
            dma((layers, 2, chunks)),
        ],
        compiler_params=pltpu.CompilerParams(
            collective_id=0, has_side_effects=True, vmem_limit_bytes=60 * 1024 * 1024
        ),
    )(features, conv_weight)


def solution(mesh):
    placed = (P("frame", "row", None, None), P())
    return jax.shard_map(
        local, mesh=mesh, in_specs=placed, out_specs=P("frame", "row", None, None), check_vma=False
    )
```

time: 75.9 us -> 33 us (0.43)
  the two profiles are of different devices: /device:TPU:14 before, /device:TPU:25 now
where the time goes in v1:
time: 33 us; the launch traced here: 32.8 us
  Pallas kernels  30.5 us (92%)
  local copies, waits for them, and re-layouts  2.29 us (7%)
    pallas_call x1, Pallas kernels, local(): pl.pallas_call(functools.partial(kernel, cuts), out_shape=jax.ShapeDtypeS...  30.5 us
    unnamed x1, local copies, waits for them, and re-layouts  2.29 us

profile of v1, /device:TPU:25, one launch (start us, length us, event | category | flops | bytes accessed | tf_op | source)
XLA Modules:
  0.0 32.8 jit_solution(12410774764439242947)
XLA Ops:
  0.0 30.5 %shard_map.28 = f32[1,4,256,256]{3,2,1,0:T(8,128)} custom-call(f32[1,4,256,256]{3,2,1,0:T(8,128)} %x_hbm.1, f32[2,3,3,256,256]{4,3,2,1,0:T(8,128)} %w_hbm.1), custom_call_target="tpu_custom_call" | custom-call | tf_op jit(solution)/shard_map/pallas_call | solution.py:276
  30.6 2.3 %copy.4 = f32[1,4,256,256]{3,2,1,0:T(8,128)} copy(f32[1,4,256,256]{3,2,1,0:T(8,128)} %shard_map.28) | data formatting | bytes 2097152

commit v2 on v1

--- a/solution.py
+++ b/solution.py
@@ -19,8 +19,8 @@
 
 
 def kernel(
-    cuts, x_hbm, w_hbm, o_hbm, xin, wbuf, w3, sx, acc, mid, halo, edge, pack, got, out,
-    load_sem, store_sem, row_send, row_recv, frame_send, frame_recv,
+    cuts, x_hbm, w_hbm, out, xin, wbuf, w3, sx, acc, mid, halo, edge, pack, got,
+    load_sem, row_send, row_recv, frame_send, frame_recv,
 ):
     rows, cols, chans = xin.shape
     layers = wbuf.shape[0]
@@ -231,8 +231,6 @@
         target = out if final else mid.at[layer]
         for row in range(1, last):
             target[row] = finish(row, 0, cols)
-            if final:
-                pltpu.make_async_copy(out.at[row], o_hbm.at[0, row], store_sem.at[row]).start()
         for chunk in range(chunks):
             outer(layer, chunk)
             start = cuts[layer + 1][chunk]
@@ -244,9 +242,6 @@
                 send_frames(layer + 1, chunk)
                 take_frames(layer + 1, chunk)
                 lower_edges(layer + 1, chunk)
-        if final:
-            for row in (0, last):
-                pltpu.make_async_copy(out.at[row], o_hbm.at[0, row], store_sem.at[row]).start()
 
     for layer in range(layers):
         for chunk in range(chunks):
@@ -261,8 +256,13 @@
                 def _():
                     frame_copy(layer, side, chunk).wait_send()
 
-    for row in range(rows):
-        pltpu.make_async_copy(out.at[row], o_hbm.at[0, row], store_sem.at[row]).wait()
+
+def store(y_ref, o_hbm, sem):
+    copies = [pltpu.make_async_copy(y_ref.at[n], o_hbm.at[0, n], sem.at[n]) for n in range(y_ref.shape[0])]
+    for copy in copies:
+        copy.start()
+    for copy in copies:
+        copy.wait()
 
 
 def local(features, conv_weight):
@@ -273,11 +273,11 @@
     chunks = len(cuts[0]) - 1
     f32, bf16 = jnp.float32, jnp.bfloat16
     dma = pltpu.SemaphoreType.DMA
-    return pl.pallas_call(
+    result = pl.pallas_call(
         functools.partial(kernel, cuts),
-        out_shape=jax.ShapeDtypeStruct(features.shape, f32),
+        out_shape=pltpu.VMEM((rows, cols, chans), f32),
         in_specs=[pl.BlockSpec(memory_space=pl.ANY)] * 2,
-        out_specs=pl.BlockSpec(memory_space=pl.ANY),
+        out_specs=pl.BlockSpec(memory_space=pltpu.VMEM),
         scratch_shapes=[
             pltpu.VMEM((rows, cols, chans), f32),
             pltpu.VMEM(conv_weight.shape, f32),
@@ -289,18 +289,24 @@
             pltpu.VMEM((layers, 2, cols, LANES), f32),
             pltpu.VMEM((layers, 2, cols, LANES), f32),
             pltpu.VMEM((layers, 2, cols, LANES), f32),
-            pltpu.VMEM((rows, cols, chans), f32),
             dma((layers + 1,)),
-            dma((rows,)),
             dma((layers, 2, 2, chunks)),
             dma((layers, 2, 2, chunks)),
             dma((layers, 2, chunks)),
             dma((layers, 2, chunks)),
         ],
         compiler_params=pltpu.CompilerParams(
-            collective_id=0, has_side_effects=True, vmem_limit_bytes=60 * 1024 * 1024
+            collective_id=0, has_side_effects=True, vmem_limit_bytes=62 * 1024 * 1024
         ),
     )(features, conv_weight)
+    return pl.pallas_call(
+        store,
+        out_shape=jax.ShapeDtypeStruct(features.shape, f32),
+        in_specs=[pl.BlockSpec(memory_space=pltpu.VMEM)],
+        out_specs=pl.BlockSpec(memory_space=pl.ANY),
+        scratch_shapes=[dma((rows,))],
+        compiler_params=pltpu.CompilerParams(vmem_limit_bytes=2 * 1024 * 1024),
+    )(result)
 
 
 def solution(mesh):

time: 33 us -> 30.9 us (0.936)
  local copies, waits for them, and re-layouts: 2.29 us -> 0 us
    unnamed x1 -> x0, local copies, waits for them, and re-layouts: 2.29 us -> none
    pallas_call x1 -> x2, Pallas kernels: 30.5 us -> 30.7 us  [the longest x1 29.7 us: local(): pl.pallas_call(functools.partial(kernel, cuts), out_shape=pltpu.VMEM((row...]
where the time goes in v2:
time: 30.9 us; the launch traced here: 30.7 us
  Pallas kernels  30.7 us (99%)
    pallas_call x1, Pallas kernels, local(): pl.pallas_call(functools.partial(kernel, cuts), out_shape=pltpu.VMEM((row...  29.7 us
    pallas_call x1, Pallas kernels, local(): pl.pallas_call(store, out_shape=jax.ShapeDtypeStruct(features.shape, f32)...  1 us

profile of v2, /device:TPU:25, one launch (start us, length us, event | category | flops | bytes accessed | tf_op | source)
XLA Modules:
  0.0 30.7 jit_solution(797705396379708037)
XLA Ops:
  0.0 29.7 %shard_map.28.y_ref = f32[4,256,256]{2,1,0:T(8,128)S(1)} custom-call(f32[1,4,256,256]{3,2,1,0:T(8,128)} %x_hbm.1, f32[2,3,3,256,256]{4,3,2,1,0:T(8,128)} %w_hbm.1), custom_call_target="tpu_custom_call" | custom-call | tf_op jit(solution)/shard_map/pallas_call | solution.py:276
  29.7 1.0 %shard_map.29 = f32[1,4,256,256]{3,2,1,0:T(8,128)} custom-call(f32[4,256,256]{2,1,0:T(8,128)S(1)} %shard_map.28.y_ref), custom_call_target="tpu_custom_call" | custom-call | tf_op jit(solution)/shard_map/pallas_call | solution.py:302

commit v3 on v2

--- a/solution.py
+++ b/solution.py
@@ -172,11 +172,17 @@
 
     def inner(layer):
         def across(tap, carry):
-            left = jnp.concatenate(
-                [sx[pl.ds(down, rows)].reshape(rows * cols, 3 * chans) for down in range(3)], axis=1
-            )
-            total = jnp.dot(left, w3[layer, tap], preferred_element_type=jnp.float32)
-            acc[tap, :, pl.ds(PAD, cols)] = total.reshape(rows, cols, chans)
+            for first, count, low, high in ((0, 1, 1, 3), (1, rows - 2, 0, 3), (last, 1, 0, 2)):
+                left = jnp.concatenate(
+                    [
+                        sx[pl.ds(first + down, count)].reshape(count * cols, 3 * chans)
+                        for down in range(low, high)
+                    ],
+                    axis=1,
+                )
+                taps = w3[layer, tap, pl.ds(low * 3 * chans, (high - low) * 3 * chans)]
+                total = jnp.dot(left, taps, preferred_element_type=jnp.float32)
+                acc[tap, pl.ds(first, count), pl.ds(PAD, cols)] = total.reshape(count, cols, chans)
             return carry
 
         lax.fori_loop(0, 3, across, 0)
@@ -212,22 +218,21 @@
 
     chunks = len(cuts[0]) - 1
     load_x.wait()
-    for chunk in range(chunks):
-        send_rows(0, 1, chunk)
+    send_rows(0, 1, 0)
     for chunk in range(chunks):
         send_frames(0, chunk)
+    split_weights(0)
     acc[:, :, pl.ds(0, PAD)] = jnp.zeros((3, rows, PAD, chans), jnp.float32)
     acc[:, :, pl.ds(PAD + cols, PAD)] = jnp.zeros((3, rows, PAD, chans), jnp.float32)
     for chunk in range(chunks):
+        if chunk > 0:
+            send_rows(0, 1, chunk)
         take_frames(0, chunk)
         lower_edges(0, chunk)
-    split_weights(0)
     for layer in range(layers):
         final = layer == layers - 1
         fill(layer)
         inner(layer)
-        if not final:
-            split_weights(layer + 1)
         target = out if final else mid.at[layer]
         for row in range(1, last):
             target[row] = finish(row, 0, cols)
@@ -240,6 +245,8 @@
             if not final:
                 send_rows(layer + 1, 1, chunk)
                 send_frames(layer + 1, chunk)
+                if chunk == 0:
+                    split_weights(layer + 1)
                 take_frames(layer + 1, chunk)
                 lower_edges(layer + 1, chunk)
 

time: 30.9 us -> 29.2 us (0.945)
  Pallas kernels: 30.7 us -> 29 us
    pallas_call x1, Pallas kernels: 29.7 us -> 28 us  [local(): pl.pallas_call(functools.partial(kernel, cuts), out_shape=pltpu.VMEM((row...]
where the time goes in v3:
time: 29.2 us; the launch traced here: 29 us
  Pallas kernels  29 us (99%)
    pallas_call x1, Pallas kernels, local(): pl.pallas_call(functools.partial(kernel, cuts), out_shape=pltpu.VMEM((row...  28 us
    pallas_call x1, Pallas kernels, local(): pl.pallas_call(store, out_shape=jax.ShapeDtypeStruct(features.shape, f32)...  1 us

profile of v3, /device:TPU:25, one launch (start us, length us, event | category | flops | bytes accessed | tf_op | source)
XLA Modules:
  0.0 29.0 jit_solution(17230659430971010677)
XLA Ops:
  0.0 28.0 %shard_map.28.y_ref = f32[4,256,256]{2,1,0:T(8,128)S(1)} custom-call(f32[1,4,256,256]{3,2,1,0:T(8,128)} %x_hbm.1, f32[2,3,3,256,256]{4,3,2,1,0:T(8,128)} %w_hbm.1), custom_call_target="tpu_custom_call" | custom-call | tf_op jit(solution)/shard_map/pallas_call | solution.py:283
  28.0 1.0 %shard_map.29 = f32[1,4,256,256]{3,2,1,0:T(8,128)} custom-call(f32[4,256,256]{2,1,0:T(8,128)S(1)} %shard_map.28.y_ref), custom_call_target="tpu_custom_call" | custom-call | tf_op jit(solution)/shard_map/pallas_call | solution.py:309
